TPU v7x, 32 devices: a whole 2x2x4 slice. The times are simulated.
32 devices in a mesh: var: 4 (over z), lon: 4 (over x, core), lat: 2 (over y).
Axes of the slice: x: 2, y: 2, z: 4, core: 2. Of those that a mesh axis runs over, the one named last changes fastest.
Arguments:
- fields: bfloat16 [48, 2, 48, 48, 16], P(('var', 'lat'), None, None, 'lon'), may hold values from -6 to 6
- score_table: bfloat16 [48, 16, 8], replicated, may hold values from -120 to 120
- score_bias: float32 [48, 8], replicated, may hold values from -6 to 6
- value_table: bfloat16 [48, 16, 512], replicated, may hold values from -1.5 to 1.5
- value_bias: float32 [48, 512], replicated, may hold values from -6 to 6
- agg_weight: bfloat16 [512, 512], replicated, may hold values from -0.25 to 0.25
- qkv_weight: bfloat16 [2, 512, 1536], replicated, may hold values from -10 to 10
- proj_weight: bfloat16 [2, 512, 512], replicated, may hold values from -0.25 to 0.25
- up_weight: bfloat16 [512, 2048], replicated, may hold values from -0.25 to 0.25
- down_weight: bfloat16 [2048, 512], replicated, may hold values from -0.125 to 0.125
- norm_gains: float32 [4, 512], replicated, may hold values from 0.1 to 1.9
- decode_weight: bfloat16 [512, 768], replicated, may hold values from -0.25 to 0.25
- decode_bias: float32 [768], replicated, may hold values from -3 to 3
Outputs:
- forecast: bfloat16 [2, 48, 48, 768], P(None, ('var', 'lat'), 'lon')
All inputs are finite; a program needn't handle non-finite values.
Results may differ from a plain program's by a relative error of at most 0.025.
Values may be sent and summed in bfloat16 or wider, within the bound.
No kernel may reach another device: no remote copies, remote signals or barrier semaphores. Data moves between devices by JAX's collectives and lax.ppermute only.
A program may use at most 128 MiB of HBM per device.

v0:
```python
import math

import jax
import jax.numpy as jnp
from jax import lax
from jax.sharding import PartitionSpec as P

WLEV = 2
WLAT = 6
WLON = 12


EPSILON = 1e-05


def padded(array, sides, width, wrap):
    for axis, dim in sides:
        size, length = (lax.axis_size(axis), array.shape[dim])
        up = [(i, (i + 1) % size) for i in range(size if wrap else size - 1)]
        down = [(j, i) for i, j in up]
        last = lax.slice_in_dim(array, length - width, length, axis=dim)
        leading = lax.slice_in_dim(array, 0, width, axis=dim)
        before = lax.ppermute(last, axis, up)
        after = lax.ppermute(leading, axis, down)
        array = jnp.concatenate([before, array, after], axis=dim)
    return array


def layer_norm(values, norm_gain):
    centre = jnp.mean(values, axis=-1, keepdims=True)
    shifted = values - centre
    spread = jnp.mean(shifted * shifted, axis=-1, keepdims=True)
    return shifted * lax.rsqrt(spread + EPSILON) * norm_gain


def var_scores(patches, score_tab, offsets):
    scores = jnp.einsum("vlrcp,vph->vlrch", patches, score_tab, preferred_element_type=jnp.float32)
    return scores + offsets[:, None, None, None, :]


def group_terms(patches, scores, top_score, table, offsets):
    levels, rows, cols, patch_size = patches.shape[1:]
    head_count = scores.shape[-1]
    width = table.shape[-1]

    def add_var(totals, pieces):
        patch, score, tab, offset = pieces
        weights = jnp.exp(score - top_score)
        values = (
            jnp.dot(patch.reshape(-1, patch_size), tab, preferred_element_type=jnp.float32) + offset
        )
        values = values.reshape(levels, rows, cols, head_count, width // head_count)
        return ((totals[0] + weights[..., None] * values, totals[1] + weights), None)

    start = (
        jnp.zeros((levels, rows, cols, head_count, width // head_count), jnp.float32),
        jnp.zeros((levels, rows, cols, head_count), jnp.float32),
    )
    sums, _ = lax.scan(add_var, start, (patches, scores, table, offsets))
    return sums


def attend(queries, keys_vals, allowed, head_count):
    windows, length, model_width = queries.shape
    head_dim = model_width // head_count
    query_heads = queries.reshape(windows, length, head_count, head_dim)
    key_heads = keys_vals[..., :model_width].reshape(windows, -1, head_count, head_dim)
    value_heads = keys_vals[..., model_width:].reshape(windows, -1, head_count, head_dim)
    scores = jnp.einsum(
        "bqhd,bkhd->bhqk", query_heads, key_heads, preferred_element_type=jnp.float32
    ) / math.sqrt(head_dim)
    if allowed is not None:
        scores = jnp.where(allowed[:, None], scores, -jnp.inf)
    scores = scores - jnp.max(scores, axis=-1, keepdims=True)
    raised = jnp.exp(scores)
    weights = (raised / jnp.sum(raised, axis=-1, keepdims=True)).astype(jnp.bfloat16)
    context = jnp.einsum(
        "bhqk,bkhd->bqhd", weights, value_heads, preferred_element_type=jnp.float32
    )
    return context.astype(jnp.bfloat16).reshape(windows, length, model_width)


def to_windows(source, window_sizes):
    level_size, row_size, col_size = window_sizes
    level_count, row_count, col_count, features = source.shape
    blocked = source.reshape(
        level_count // level_size,
        level_size,
        row_count // row_size,
        row_size,
        col_count // col_size,
        col_size,
        features,
    )
    blocked = blocked.transpose(0, 2, 4, 1, 3, 5, 6)
    return blocked.reshape(-1, level_size * row_size * col_size, features)


def from_windows(windowed, full_shape, window_sizes):
    level_size, row_size, col_size = window_sizes
    level_count, row_count, col_count, features = full_shape
    blocked = windowed.reshape(
        level_count // level_size,
        row_count // row_size,
        col_count // col_size,
        level_size,
        row_size,
        col_size,
        features,
    )
    return blocked.transpose(0, 3, 1, 4, 2, 5, 6).reshape(full_shape)


def per_device(
    fields,
    score_table,
    score_bias,
    value_table,
    value_bias,
    agg_weight,
    qkv_weight,
    proj_weight,
    up_weight,
    down_weight,
    norm_gains,
    decode_weight,
    decode_bias,
):
    groups = lax.axis_size(("var", "lat"))
    band_index = lax.axis_index(("var", "lat"))
    local_vars, levels, all_rows, band_cols, patch_size = fields.shape
    band_rows = all_rows // groups
    head_count = score_table.shape[2]
    model_width = agg_weight.shape[0]
    first_var = band_index * local_vars
    own_scores = lax.dynamic_slice_in_dim(score_table, first_var, local_vars, 0)
    own_offsets = lax.dynamic_slice_in_dim(score_bias, first_var, local_vars, 0)
    own_values = lax.dynamic_slice_in_dim(value_table, first_var, local_vars, 0)
    own_biases = lax.dynamic_slice_in_dim(value_bias, first_var, local_vars, 0)
    scores = var_scores(fields, own_scores, own_offsets)
    top_score = lax.pmax(jnp.max(scores, axis=0).astype(jnp.bfloat16), ("var", "lat")).astype(
        jnp.float32
    )
    numerator, denominator = group_terms(fields, scores, top_score, own_values, own_biases)
    numerator = numerator.reshape(levels, all_rows, band_cols, model_width)
    numerator, denominator = (
        lax.psum(numerator.astype(jnp.bfloat16), ("var", "lat")).astype(jnp.float32),
        lax.psum(denominator.astype(jnp.bfloat16), ("var", "lat")).astype(jnp.float32),
    )
    numerator = lax.dynamic_slice_in_dim(numerator, band_index * band_rows, band_rows, 1)
    denominator = lax.dynamic_slice_in_dim(denominator, band_index * band_rows, band_rows, 1)
    pooled = (
        numerator.reshape(levels, band_rows, band_cols, head_count, -1) / denominator[..., None]
    )
    pooled = pooled.reshape(levels, band_rows, band_cols, model_width).astype(jnp.bfloat16)
    latent = jnp.dot(pooled, agg_weight, preferred_element_type=jnp.float32)
    sizes = (WLEV, WLAT, WLON)
    normed = layer_norm(latent, norm_gains[0]).astype(jnp.bfloat16)
    projected = jnp.dot(normed, qkv_weight[0], preferred_element_type=jnp.float32).astype(
        jnp.bfloat16
    )
    windowed = to_windows(projected, sizes)
    context = attend(windowed[..., :model_width], windowed[..., model_width:], None, head_count)
    context = from_windows(context, (levels, band_rows, band_cols, model_width), sizes)
    hidden = latent + jnp.dot(context, proj_weight[0], preferred_element_type=jnp.float32)
    mixed = layer_norm(hidden, norm_gains[1]).astype(jnp.bfloat16)
    active = jax.nn.gelu(
        jnp.dot(mixed, up_weight, preferred_element_type=jnp.float32), approximate=True
    ).astype(jnp.bfloat16)
    latent = hidden + jnp.dot(active, down_weight, preferred_element_type=jnp.float32)
    level_half, row_half, col_half = (WLEV // 2, WLAT // 2, WLON // 2)
    normed = layer_norm(latent, norm_gains[2]).astype(jnp.bfloat16)
    query_weight = qkv_weight[1][:, :model_width]
    pair_weight = qkv_weight[1][:, model_width:]
    queries = jnp.dot(normed, query_weight, preferred_element_type=jnp.float32).astype(jnp.bfloat16)
    tall_frame = padded(normed, ((("var", "lat"), 1),), row_half, False)
    framed = padded(tall_frame, (("lon", 2),), col_half, True)
    framed = jnp.dot(framed, pair_weight, preferred_element_type=jnp.float32).astype(jnp.bfloat16)
    frame_rows = band_rows + 2 * row_half
    frame_cols = band_cols + 2 * col_half
    padded_queries = jnp.pad(queries, ((0, 0), (row_half, row_half), (col_half, col_half), (0, 0)))
    level_ids = (jnp.arange(levels) + level_half) // WLEV
    global_rows = band_index * band_rows + jnp.arange(frame_rows) - row_half
    valid_rows = ((global_rows >= 0) & (global_rows < groups * band_rows)).astype(jnp.int32)
    grid_shape = (levels, frame_rows, frame_cols, 1)
    level_grid = jnp.broadcast_to(level_ids[:, None, None, None], grid_shape)
    valid_grid = jnp.broadcast_to(valid_rows[None, :, None, None], grid_shape)
    level_windows = to_windows(jnp.roll(level_grid, -level_half, axis=0), sizes)[..., 0]
    valid_windows = to_windows(jnp.roll(valid_grid, -level_half, axis=0), sizes)[..., 0]
    allowed = (level_windows[:, :, None] == level_windows[:, None, :]) & (
        valid_windows[:, None, :] == 1
    )
    query_windows = to_windows(jnp.roll(padded_queries, -level_half, axis=0), sizes)
    pair_windows = to_windows(jnp.roll(framed, -level_half, axis=0), sizes)
    context = attend(query_windows, pair_windows, allowed, head_count)
    context = from_windows(context, (levels, frame_rows, frame_cols, model_width), sizes)
    context = jnp.roll(context, level_half, axis=0)[
        :, row_half : row_half + band_rows, col_half : col_half + band_cols
    ]
    latent = latent + jnp.dot(context, proj_weight[1], preferred_element_type=jnp.float32)
    final = layer_norm(latent, norm_gains[3]).astype(jnp.bfloat16)
    return (jnp.dot(final, decode_weight, preferred_element_type=jnp.float32) + decode_bias).astype(
        jnp.bfloat16
    )


def solution(mesh):
    return jax.shard_map(
        per_device,
        mesh=mesh,
        in_specs=(
            P(("var", "lat"), None, None, "lon", None),
            P(),
            P(),
            P(),
            P(),
            P(),
            P(),
            P(),
            P(),
            P(),
            P(),
            P(),
            P(),
        ),
        out_specs=P(None, ("var", "lat"), "lon", None),
        check_vma=False,
    )
```

profile of v0, /device:TPU:11, one launch (start us, length us, event | category | flops | bytes accessed | tf_op | source)
XLA Modules:
  0.0 317.7 jit_solution(7417999574103938440)
XLA Ops:
  6.5 1.0 constant_dynamic-slice_fusion.6
  8.5 2.1 fusion.98
  10.6 27.8 %pmax.7 = bf16[2,48,12,8]{1,3,2,0:T(8,128)(2,1)S(1)} all-reduce(bf16[2,48,12,8]{1,3,2,0:T(8,128)(2,1)S(1)} %get-tuple-element.148), channel_id=1, replica_groups=mesh['var'=4,'lon'=4,'lat'=2] {'var','lat'}, use_global_device_ids=true, to_apply=%region_1.0 | all-reduce | flops 9216 | bytes 36864 | tf_op jit(solution)/shard_map/pmax | solution.py:141
  38.5 1.2 copy.81
  41.3 105.9 %while.13 = (s32[]{:T(128)}, f32[2,48,12,8,64]{4,3,2,1,0:T(8,128)}, f32[2,48,12,8]{3,2,1,0:T(8,128)}, f32[6,2,48,12,8]{2,4,3,1,0:T(8,128)}, f32[2,48,12,8]{3,2,1...) while((s32[]{:T(128)}, f32[2,48,12,8,64]{4,3,2,1,0:T(8,128)}, ...), condition=%wide.region_3.4_spmd.clone, body=%wide.region_2.3_spmd.clone.sunk | while | flops 21261312 | bytes 14805120 | solution.py:59
  43.1 1.9 convolution_add_fusion.6
  45.0 4.6 %reshape.245 = f32[2,48,12,8,64]{4,3,2,1,0:T(8,128)} reshape(f32[1152,512]{1,0:T(8,128)} %convolution_add_fusion.6) | data formatting | bytes 4718592 | tf_op jit(solution)/shard_map/while/body/eval_jaxpr/reshape | solution.py:52
  50.8 2.2 select_add_fusion.4
  53.1 4.6 %select_add_fusion.5 = f32[2,48,12,8,64]{4,3,2,1,0:T(8,128)} fusion(f32[2,48,12,8,64]{4,3,2,1,0:T(8,128)} %get-tuple-element.226, f32[2,48,12,8,64]{4,3,2,1,0:T(8,128)} %reshape.245, f32[2,48,12,8]{3,2,1,0:T(8,128)S(1)} %get-tuple-element.213, pred[]{:T(512)S(6)} %compare.15), kind=kLoop, calls=%fused_computation.clone.1 | loop fusion | flops 1769472 | bytes 7114753 | tf_op jit(solution)/shard_map/while/body/eval_jaxpr/add | solution.py:53
  59.4 1.9 convolution_add_fusion.6
  61.3 4.6 %reshape.245 = f32[2,48,12,8,64]{4,3,2,1,0:T(8,128)} reshape(f32[1152,512]{1,0:T(8,128)} %convolution_add_fusion.6) | data formatting | bytes 4718592 | tf_op jit(solution)/shard_map/while/body/eval_jaxpr/reshape | solution.py:52
  67.1 2.5 select_add_fusion.4
  69.6 5.9 %select_add_fusion.5 = f32[2,48,12,8,64]{4,3,2,1,0:T(8,128)} fusion(f32[2,48,12,8,64]{4,3,2,1,0:T(8,128)} %get-tuple-element.226, f32[2,48,12,8,64]{4,3,2,1,0:T(8,128)} %reshape.245, f32[2,48,12,8]{3,2,1,0:T(8,128)S(1)} %get-tuple-element.213, pred[]{:T(512)S(6)} %compare.15), kind=kLoop, calls=%fused_computation.clone.1 | loop fusion | flops 1769472 | bytes 7114753 | tf_op jit(solution)/shard_map/while/body/eval_jaxpr/add | solution.py:53
  77.3 1.9 convolution_add_fusion.6
  79.2 4.6 %reshape.245 = f32[2,48,12,8,64]{4,3,2,1,0:T(8,128)} reshape(f32[1152,512]{1,0:T(8,128)} %convolution_add_fusion.6) | data formatting | bytes 4718592 | tf_op jit(solution)/shard_map/while/body/eval_jaxpr/reshape | solution.py:52
  85.1 2.5 select_add_fusion.4
  87.5 5.9 %select_add_fusion.5 = f32[2,48,12,8,64]{4,3,2,1,0:T(8,128)} fusion(f32[2,48,12,8,64]{4,3,2,1,0:T(8,128)} %get-tuple-element.226, f32[2,48,12,8,64]{4,3,2,1,0:T(8,128)} %reshape.245, f32[2,48,12,8]{3,2,1,0:T(8,128)S(1)} %get-tuple-element.213, pred[]{:T(512)S(6)} %compare.15), kind=kLoop, calls=%fused_computation.clone.1 | loop fusion | flops 1769472 | bytes 7114753 | tf_op jit(solution)/shard_map/while/body/eval_jaxpr/add | solution.py:53
  95.2 1.9 convolution_add_fusion.6
  97.1 4.6 %reshape.245 = f32[2,48,12,8,64]{4,3,2,1,0:T(8,128)} reshape(f32[1152,512]{1,0:T(8,128)} %convolution_add_fusion.6) | data formatting | bytes 4718592 | tf_op jit(solution)/shard_map/while/body/eval_jaxpr/reshape | solution.py:52
  103.0 2.5 select_add_fusion.4
  105.5 5.9 %select_add_fusion.5 = f32[2,48,12,8,64]{4,3,2,1,0:T(8,128)} fusion(f32[2,48,12,8,64]{4,3,2,1,0:T(8,128)} %get-tuple-element.226, f32[2,48,12,8,64]{4,3,2,1,0:T(8,128)} %reshape.245, f32[2,48,12,8]{3,2,1,0:T(8,128)S(1)} %get-tuple-element.213, pred[]{:T(512)S(6)} %compare.15), kind=kLoop, calls=%fused_computation.clone.1 | loop fusion | flops 1769472 | bytes 7114753 | tf_op jit(solution)/shard_map/while/body/eval_jaxpr/add | solution.py:53
  113.1 1.9 convolution_add_fusion.6
  115.0 4.6 %reshape.245 = f32[2,48,12,8,64]{4,3,2,1,0:T(8,128)} reshape(f32[1152,512]{1,0:T(8,128)} %convolution_add_fusion.6) | data formatting | bytes 4718592 | tf_op jit(solution)/shard_map/while/body/eval_jaxpr/reshape | solution.py:52
  120.9 2.5 select_add_fusion.4
  123.4 5.9 %select_add_fusion.5 = f32[2,48,12,8,64]{4,3,2,1,0:T(8,128)} fusion(f32[2,48,12,8,64]{4,3,2,1,0:T(8,128)} %get-tuple-element.226, f32[2,48,12,8,64]{4,3,2,1,0:T(8,128)} %reshape.245, f32[2,48,12,8]{3,2,1,0:T(8,128)S(1)} %get-tuple-element.213, pred[]{:T(512)S(6)} %compare.15), kind=kLoop, calls=%fused_computation.clone.1 | loop fusion | flops 1769472 | bytes 7114753 | tf_op jit(solution)/shard_map/while/body/eval_jaxpr/add | solution.py:53
  131.1 1.9 convolution_add_fusion.6
  133.0 4.6 %reshape.245 = f32[2,48,12,8,64]{4,3,2,1,0:T(8,128)} reshape(f32[1152,512]{1,0:T(8,128)} %convolution_add_fusion.6) | data formatting | bytes 4718592 | tf_op jit(solution)/shard_map/while/body/eval_jaxpr/reshape | solution.py:52
  138.8 2.5 select_add_fusion.4
  141.3 5.9 %select_add_fusion.5 = f32[2,48,12,8,64]{4,3,2,1,0:T(8,128)} fusion(f32[2,48,12,8,64]{4,3,2,1,0:T(8,128)} %get-tuple-element.226, f32[2,48,12,8,64]{4,3,2,1,0:T(8,128)} %reshape.245, f32[2,48,12,8]{3,2,1,0:T(8,128)S(1)} %get-tuple-element.213, pred[]{:T(512)S(6)} %compare.15), kind=kLoop, calls=%fused_computation.clone.1 | loop fusion | flops 1769472 | bytes 7114753 | tf_op jit(solution)/shard_map/while/body/eval_jaxpr/add | solution.py:53
  147.2 4.2 %convert_element_type.84 = bf16[2,48,12,8,64]{4,3,2,1,0:T(8,128)(2,1)} convert(f32[2,48,12,8,64]{4,3,2,1,0:T(8,128)} %get-tuple-element.48) | non-fusion elementwise | flops 589824 | bytes 3538944 | tf_op jit(solution)/shard_map/convert_element_type | solution.py:147
  151.4 4.4 %reshape.241 = bf16[2,48,12,512]{3,2,1,0:T(8,128)(2,1)} reshape(bf16[2,48,12,8,64]{4,3,2,1,0:T(8,128)(2,1)} %convert_element_type.84) | data formatting | bytes 2359296 | tf_op jit(solution)/shard_map/convert_element_type | solution.py:147
  155.8 3.2 copy.117
  159.1 34.6 %psum.15 = bf16[2,48,12,8]{3,2,1,0:T(8,128)(2,1)S(1)} all-reduce(bf16[2,48,12,8]{3,2,1,0:T(8,128)(2,1)S(1)} %convert_element_type.87), channel_id=1, replica_groups=mesh['var'=4,'lon'=4,'lat'=2] {'var','lat'}, use_global_device_ids=true, to_apply=%region_5.6 | all-reduce | flops 9216 | bytes 36864 | tf_op jit(solution)/shard_map/psum | solution.py:148
  195.2 1.3 concatenate.28
  197.5 2.7 slice_bitcast_fusion
  200.2 49.8 %all-reduce.4.cloned.1.call-done = bf16[2,48,12,512]{3,1,2,0:T(8,128)(2,1)} async-done(((bf16[2,48,12,512]{3,1,2,0:T(8,128)(2,1)}), bf16[2,48,12,512]{3,1,2,0:T(8,128)(2,1)}) %all-reduce.4.cloned.1.call-update) | async-done | bytes 1179664 | tf_op jit(solution)/shard_map/psum | solution.py:147
  250.0 1.2 fusion.63
  251.7 1.9 convolution_convert_fusion
  255.0 1.6 fusion.100
  256.5 1.5 fusion.40
  258.5 1.4 fusion.101
  260.1 3.0 fusion.102
  263.5 3.0 collective-permute-start
  266.5 3.2 %collective-permute-start.1 = (bf16[2,3,12,512]{3,2,1,0:T(8,128)(2,1)S(1)}, bf16[2,3,12,512]{3,2,1,0:T(8,128)(2,1)S(1)}, u32[]{:S(2)}, u32[]{:S(2)}) collective-permute-start(bf16[2,3,12,512]{3,2,1,0:T(8,128)(2,1)S(1)} %get-tuple-element.141), channel_id=1, source_target_pairs={{1,0},{8,1},{9,8},{16,9},{17,16},{24,17},{25,24},{3,2},{10,3},{11,... | collective-permute-start | bytes 221192 | tf_op jit(solution)/shard_map/ppermute | solution.py:24
  269.7 1.3 convolution_convert_fusion.3
  271.0 1.5 collective-permute-done.1
  272.7 2.3 collective-permute-start.2
  276.3 1.7 reshape_reshape.6
  278.1 3.4 %collective-permute-done.3 = bf16[2,12,6,512]{3,2,1,0:T(8,128)(2,1)} collective-permute-done((bf16[2,12,6,512]{3,2,1,0:T(8,128)(2,1)S(1)}, bf16[2,12,6,512]{3,2,1,0:T(8,128)(2,1)}, u32[]{:S(2)}, u32[]{:S(2)}) %collective-permute-start.3) | collective-permute-done | bytes 147488 | tf_op jit(solution)/shard_map/ppermute | solution.py:24
  281.5 2.2 convolution_convert_fusion.1
  283.9 1.2 copy.92
  285.1 2.2 copy.93
  287.3 3.2 reshape.225
  290.5 1.4 fusion.90
  292.0 2.3 copy.98
  294.3 2.2 copy.94
  296.5 2.1 fusion.38
  298.7 1.6 fusion.105
  300.3 1.5 fusion.32
  301.8 2.1 copy.101
  303.9 1.4 reshape_reshape.7
  305.3 1.5 fusion.92
  307.9 1.5 fusion.106
  310.0 0.9 copy.104
  (124 shorter events, 29.2 us)
Async XLA Ops:
  6.5 253.6 %copy-start = (bf16[2048,512]{1,0:T(8,128)(2,1)S(1)}, bf16[2048,512]{1,0:T(8,128)(2,1)}, u32[]{:S(2)}) copy-start(bf16[2048,512]{1,0:T(8,128)(2,1)} %param.24) | copy-start | bytes 6291460
  6.5 243.4 %all-reduce.4.cloned.1.call-start = ((), (), s32[]{:S(2)}) async-start(), calls=%async_computation | async-start | bytes 2359296 | tf_op jit(solution)/shard_map/psum | solution.py:147
  155.8 3.2 %copy-start.1 = (f32[2,48,12,8]{3,2,1,0:T(8,128)S(1)}, f32[2,48,12,8]{3,2,1,0:T(8,128)}, u32[]{:S(2)}) copy-start(f32[2,48,12,8]{3,2,1,0:T(8,128)} %get-tuple-element.49) | copy-start | bytes 110596
  159.1 37.5 %copy-start.10 = (f32[4,512]{1,0:T(4,128)S(1)}, f32[4,512]{1,0:T(4,128)}, u32[]{:S(2)}) copy-start(f32[4,512]{1,0:T(4,128)} %param.25) | copy-start | bytes 24580
  197.5 53.7 %copy-start.7 = (bf16[512,512]{1,0:T(8,128)(2,1)S(1)}, bf16[512,512]{1,0:T(8,128)(2,1)}, u32[]{:S(2)}) copy-start(bf16[512,512]{1,0:T(8,128)(2,1)} %param.20) | copy-start | bytes 1572868
  255.0 1.6 copy-start.8
  263.1 9.5 %copy-start.3 = (f32[2,6,12,512]{3,2,1,0:T(8,128)}, f32[2,6,12,512]{3,2,1,0:T(8,128)S(1)}, u32[]{:S(2)}) copy-start(f32[2,6,12,512]{3,2,1,0:T(8,128)S(1)} %get-tuple-element.157) | copy-start | bytes 884740
  263.5 7.5 %collective-permute-start = (bf16[2,3,12,512]{3,2,1,0:T(8,128)(2,1)S(1)}, bf16[2,3,12,512]{3,2,1,0:T(8,128)(2,1)S(1)}, u32[]{:S(2)}, u32[]{:S(2)}) collective-permute-start(bf16[2,3,12,512]{3,2,1,0:T(8,128)(2,1)S(1)} %get-tuple-element.140), channel_id=1, source_target_pairs={{0,1},{1,8},{8,9},{9,16},{16,17},{17,24},{24,25},{2,3},{3,10},{10,... | collective-permute-start | bytes 221192 | tf_op jit(solution)/shard_map/ppermute | solution.py:23
  266.5 6.0 %collective-permute-start.1 = (bf16[2,3,12,512]{3,2,1,0:T(8,128)(2,1)S(1)}, bf16[2,3,12,512]{3,2,1,0:T(8,128)(2,1)S(1)}, u32[]{:S(2)}, u32[]{:S(2)}) collective-permute-start(bf16[2,3,12,512]{3,2,1,0:T(8,128)(2,1)S(1)} %get-tuple-element.141), channel_id=1, source_target_pairs={{1,0},{8,1},{9,8},{16,9},{17,16},{24,17},{25,24},{3,2},{10,3},{11,... | collective-permute-start | bytes 221192 | tf_op jit(solution)/shard_map/ppermute | solution.py:24
  272.7 5.4 %collective-permute-start.2 = (bf16[2,12,6,512]{3,2,1,0:T(8,128)(2,1)S(1)}, bf16[2,12,6,512]{3,2,1,0:T(8,128)(2,1)}, u32[]{:S(2)}, u32[]{:S(2)}) collective-permute-start(bf16[2,12,6,512]{3,2,1,0:T(8,128)(2,1)S(1)} %get-tuple-element.136), channel_id=1, source_target_pairs={{0,2},{2,4},{4,6},{6,0},{1,3},{3,5},{5,7},{7,1},{8,10},{10,12},{12... | collective-permute-start | bytes 442376 | tf_op jit(solution)/shard_map/ppermute | solution.py:23
  275.0 6.5 %collective-permute-start.3 = (bf16[2,12,6,512]{3,2,1,0:T(8,128)(2,1)S(1)}, bf16[2,12,6,512]{3,2,1,0:T(8,128)(2,1)}, u32[]{:S(2)}, u32[]{:S(2)}) collective-permute-start(bf16[2,12,6,512]{3,2,1,0:T(8,128)(2,1)S(1)} %get-tuple-element.137), channel_id=1, source_target_pairs={{2,0},{4,2},{6,4},{0,6},{3,1},{5,3},{7,5},{1,7},{10,8},{12,10},{14... | collective-permute-start | bytes 442376 | tf_op jit(solution)/shard_map/ppermute | solution.py:24
  292.0 4.6 %copy-start.2 = (bf16[4,144,8,64]{3,2,0,1:T(8,128)(2,1)S(1)}, bf16[4,144,8,64]{3,2,0,1:T(8,128)(2,1)}, u32[]{:S(2)}) copy-start(bf16[4,144,8,64]{3,2,0,1:T(8,128)(2,1)} %reshape_reshape.6) | copy-start | bytes 1769476
  296.5 2.1 copy-start.9
  298.6 1.7 copy-start.5
  306.9 1.0 copy-start.4
  307.1 2.4 copy-start.11
  307.9 1.7 copy-start.6
Sparse Core Ops, SparseCore 0:
  159.1 90.7 all-reduce.3
where the time goes:
time: 321 us; the launch traced here: 318 us
  local copies, waits for them, and re-layouts  87.7 us (27%)
  blocking collectives  62.4 us (19%)
  other arithmetic  58 us (18%)
  waiting for transfers between devices  54.7 us (17%)
  matrix products  32.2 us (10%)
  between operations  14 us (4%)
  starting transfers between devices  8.62 us (3%)
    psum x1, waiting for transfers between devices, per_device(): lax.psum(numerator.astype(jnp.bfloat16), ('var', 'lat')).astype(jnp.float32)  49.8 us
    psum x1, blocking collectives, per_device(): lax.psum(denominator.astype(jnp.bfloat16), ('var', 'lat'))  34.6 us
    add x6, other arithmetic, add_var(): totals[0] + weights[..., None] * values  34.3 us
    pmax x1, blocking collectives, per_device(): lax.pmax(jnp.max(scores, axis=0).astype(jnp.bfloat16), ('var', 'lat'))  27.8 us
    reshape x6, local copies, waits for them, and re-layouts, add_var(): values = values.reshape(levels, rows, cols, head_count, width // head_count)  27.4 us
    dynamic_slice x30, local copies, waits for them, and re-layouts, group_terms(): sums, _ = lax.scan(add_var, start, (patches, scores, table, offsets))  15.1 us
    add x6, other arithmetic, add_var(): totals[1] + weights  14.6 us
    dot_general x6, matrix products, add_var(): jnp.dot(patch.reshape(-1, patch_size), tab, preferred_element_type=jnp.fl...  11.3 us
  transfers between devices with their start and end apart: 5, of which 3 were waited for; matrix products, arithmetic and copies ran while one was open for 3% of the time, Pallas kernels for 0%

commit v1 on v0

v1 whole, which is shorter than its diff:
```python
import functools

import jax
import jax.numpy as jnp
from jax import lax
from jax.experimental import pallas as pl
from jax.experimental.pallas import tpu as pltpu
from jax.sharding import PartitionSpec as P

WLEV = 2
WLAT = 6
WLON = 12
HALF_ROWS = WLAT // 2
HALF_COLS = WLON // 2
EPSILON = 1e-05
LANES = 128
BIAS_PARTS = 3
MASKED = -1e30
F32 = jnp.float32
BF16 = jnp.bfloat16


def iota(shape, dim):
    return lax.broadcasted_iota(jnp.int32, shape, dim)


def mm(a, b):
    return lax.dot_general(a, b, (((1,), (0,)), ((), ())), preferred_element_type=F32)


def mm_nt(a, b):
    return lax.dot_general(a, b, (((1,), (1,)), ((), ())), preferred_element_type=F32)


def three_parts(values):
    parts = []
    for _ in range(BIAS_PARTS):
        part = values.astype(BF16).astype(F32)
        parts.append(part)
        values = values - part
    return parts


def layer_norm(values, gain):
    centre = jnp.mean(values, axis=-1, keepdims=True)
    shifted = values - centre
    spread = jnp.mean(shifted * shifted, axis=-1, keepdims=True)
    return shifted * lax.rsqrt(spread + EPSILON) * gain


def attend(queries, keys, values, allowed, head_count):
    width = queries.shape[1]
    head_dim = width // head_count
    pairs = []
    low = iota((1, LANES), 1) < head_dim
    scaled = queries * jnp.asarray(head_dim**-0.5, BF16)
    for start in range(0, width, LANES):
        q = scaled[:, start : start + LANES]
        k = keys[:, start : start + LANES]
        v = values[:, start : start + LANES]
        outs = []
        for side in (low, ~low):
            scores = mm_nt(jnp.where(side, q, jnp.zeros_like(q)), k)
            if allowed is not None:
                scores = jnp.where(allowed, scores, MASKED)
            raised = jnp.exp(scores - jnp.max(scores, axis=-1, keepdims=True))
            weights = raised * (1.0 / jnp.sum(raised, axis=-1, keepdims=True))
            outs.append(mm(weights.astype(BF16), v))
        pairs.append(jnp.where(low, outs[0], outs[1]).astype(BF16))
    return jnp.concatenate(pairs, axis=1)


def pack_kernel(fields_ref, out_ref, scratch_ref):
    var_count, levels, cols, patch, rows = fields_ref.shape
    bands = out_ref.shape[0]
    features = var_count * patch
    half_cols = cols // HALF_COLS
    half_rows = rows // bands // HALF_ROWS
    run = HALF_ROWS * HALF_COLS
    block = levels * run
    row_ids = iota((rows * HALF_COLS, rows), 0)
    col_ids = iota((rows * HALF_COLS, rows), 1)
    wanted = (row_ids // run) * HALF_ROWS + (row_ids % run) // HALF_COLS
    picks = [
        ((row_ids % HALF_COLS == step) & (wanted == col_ids)).astype(F32).astype(BF16)
        for step in range(HALF_COLS)
    ]
    scratch_ref[...] = jnp.ones(scratch_ref.shape, F32)
    for level in range(levels):
        for col in range(half_cols):
            total = None
            for step in range(HALF_COLS):
                tile = fields_ref[:, level, col * HALF_COLS + step].reshape(features, rows)
                part = mm_nt(picks[step], tile)
                total = part if total is None else total + part
            for band in range(bands):
                for row in range(half_rows):
                    source = (band * half_rows + row) * run
                    target = (row * half_cols + col) * block + level * run
                    scratch_ref[band, target : target + run, :features] = total[source : source + run]
    for band in range(bands):
        out_ref[band] = scratch_ref[band].astype(BF16)


def feature_var(index, local_vars, patch):
    features = local_vars * patch
    result = jnp.where(index < features, index // patch, 0)
    for part in range(BIAS_PARTS):
        first = features + part * local_vars
        result = jnp.where((index >= first) & (index < first + local_vars), index - first, result)
    return result


def pool(received_ref, table_rows, table_bias, value_ref, value_bias_ref, spread_ref, score_ref, part_ref, head_count):
    bands, cells, lanes = received_ref.shape
    all_vars = value_bias_ref.shape[0]
    width = value_bias_ref.shape[1]
    local_vars = all_vars // bands
    patch = table_rows.shape[0] // head_count
    features = local_vars * patch
    used = features + BIAS_PARTS * local_vars

    bias_rows = jnp.concatenate(three_parts(table_bias), axis=0).astype(BF16)
    stacked = jnp.concatenate([table_rows, bias_rows], axis=0)
    depth = stacked.shape[0]
    row = iota((bands * lanes, all_vars), 0)
    owner = (row // lanes) * local_vars + feature_var(row % lanes, local_vars, patch)
    picks = ((owner == iota((bands * lanes, all_vars), 1)) & (row % lanes < used)).astype(F32).astype(BF16)
    row = iota((bands * lanes, depth), 0) % lanes
    slot = jnp.where(row < features, row % patch, patch + (row - features) // local_vars)
    chosen = (iota((bands * lanes, depth), 1) // head_count) == slot
    table = jnp.where(chosen, mm_nt(picks, stacked), 0.0).astype(BF16)
    width_out = head_count * lanes
    sel = (iota((depth, width_out), 0) % head_count == iota((depth, width_out), 1) // lanes).astype(F32).astype(BF16)
    same = feature_var(iota((lanes, lanes), 0), local_vars, patch) == feature_var(
        iota((lanes, lanes), 1), local_vars, patch
    )
    same = jnp.concatenate([same.astype(F32)] * head_count, axis=1)
    for band in range(bands):
        rows = slice(band * lanes, (band + 1) * lanes)
        spread_ref[rows, :] = (mm(table[rows], sel) * same).astype(BF16)

    for band in range(bands):
        biases = value_bias_ref[band * local_vars : (band + 1) * local_vars, :]
        part_ref[...] = jnp.zeros(part_ref.shape, F32)
        for index, part in enumerate(three_parts(biases)):
            part_ref[index * local_vars : (index + 1) * local_vars, :] = part
        value_ref[band * lanes + features : (band + 1) * lanes, :] = part_ref[...].astype(BF16)

    tops = None
    for band in range(bands):
        scores = mm(received_ref[band], spread_ref[band * lanes : (band + 1) * lanes, :])
        score_ref[band] = scores
        tops = scores if tops is None else jnp.maximum(tops, scores)

    group = 2
    row = iota((group * lanes, lanes), 0) % lanes
    ones = ((row >= features) & (row < features + local_vars)).astype(F32).astype(BF16)
    head_dim = width // head_count
    low = iota((1, lanes), 1) < head_dim
    pooled = []
    for start in range(0, width, lanes):
        outs = []
        for side in range(2):
            head = start // head_dim + side
            columns = slice(head * lanes, (head + 1) * lanes)
            top = jnp.max(tops[:, columns], axis=-1, keepdims=True)
            total = None
            for first in range(0, bands, group):
                terms = [
                    (jnp.exp(score_ref[band, :, columns] - top) * received_ref[band].astype(F32)).astype(BF16)
                    for band in range(first, first + group)
                ]
                right = jnp.concatenate(
                    [value_ref[first * lanes : (first + group) * lanes, start : start + lanes], ones], axis=1
                )
                part = mm(jnp.concatenate(terms, axis=1), right)
                total = part if total is None else total + part
            outs.append(total[:, :lanes] * (1.0 / total[:, lanes:]))
        pooled.append(jnp.where(low, outs[0], outs[1]).astype(BF16))
    return jnp.concatenate(pooled, axis=1)


def first_kernel(
    received_ref, table_ref, table_bias_ref, value_bias_ref, gains_ref,
    value_hbm, agg_hbm, qkv_hbm, proj_hbm, up_hbm, down_hbm,
    normed_ref, latent_ref, l1_ref, l2_ref, s1_ref, s2_ref, c11_ref, c12_ref, c21_ref, c22_ref,
    spread_ref, score_ref, part_ref, value_ref, agg_ref, qkv_ref, proj_ref, up_ref, down_ref, own_ref, sems,
    *, levels, half_rows, half_cols, head_count, lon_axis, band_axes,
):
    bands, cells, lanes = received_ref.shape
    local_features = value_hbm.shape[0] // bands
    copies = [
        pltpu.make_async_copy(
            value_hbm.at[pl.ds(band * local_features, local_features)],
            value_ref.at[pl.ds(band * lanes, local_features)],
            sems.at[5 + band],
        )
        for band in range(bands)
    ]
    pairs = (
        (agg_hbm, agg_ref),
        (qkv_hbm.at[0], qkv_ref),
        (proj_hbm.at[0], proj_ref),
        (up_hbm, up_ref),
        (down_hbm, down_ref),
    )
    weights = [pltpu.make_async_copy(a, b, sems.at[i]) for i, (a, b) in enumerate(pairs)]
    for copy in copies + weights:
        copy.start()
    for copy in copies:
        copy.wait()
    width = agg_hbm.shape[0]
    pooled = pool(
        received_ref, table_ref[...], table_bias_ref[...], value_ref, value_bias_ref, spread_ref, score_ref, part_ref,
        head_count,
    )
    weights[0].wait()
    latent = mm(pooled, agg_ref[...])
    normed = layer_norm(latent, gains_ref[0:1, :]).astype(BF16)
    weights[1].wait()
    qkv = mm(normed, qkv_ref[...]).astype(BF16)
    block = levels * HALF_ROWS * HALF_COLS
    allowed = None
    if half_rows > 2 or half_cols > 2 or levels > WLEV:

        def window(index):
            place = index // block
            level = (index % block) // (HALF_ROWS * HALF_COLS)
            return ((place // half_cols // 2) * half_cols + place % half_cols // 2) * levels + level // WLEV

        allowed = window(iota((cells, cells), 0)) == window(iota((cells, cells), 1))
    context = attend(qkv[:, :width], qkv[:, width : 2 * width], qkv[:, 2 * width :], allowed, head_count)
    weights[2].wait()
    hidden = latent + mm(context, proj_ref[...])
    mixed = layer_norm(hidden, gains_ref[1:2, :]).astype(BF16)
    weights[3].wait()
    active = jax.nn.gelu(mm(mixed, up_ref[...]), approximate=True).astype(BF16)
    weights[4].wait()
    latent = hidden + mm(active, down_ref[...])
    latent_ref[...] = latent
    own = layer_norm(latent, gains_ref[2:3, :])
    normed_ref[...] = own.astype(BF16)
    own_ref[...] = own

    lon_even = lax.axis_index(lon_axis) % 2 == 0
    band_even = lax.axis_index(band_axes) % 2 == 0

    def cut(row, col):
        start = (row * half_cols + col) * block
        return own_ref[start : start + block, :]

    last_row, last_col = half_rows - 1, half_cols - 1
    for row in range(half_rows):
        left, right = cut(row, 0), cut(row, last_col)
        rows = slice(row * block, (row + 1) * block)
        own_ref_rows = (jnp.where(lon_even, right, left), jnp.where(lon_even, left, right))
        score_ref[0, rows, :width] = own_ref_rows[0]
        score_ref[1, rows, :width] = own_ref_rows[1]
    l1_ref[...] = score_ref[0, : half_rows * block, :width].astype(BF16)
    l2_ref[...] = score_ref[1, : half_rows * block, :width].astype(BF16)
    for col in range(half_cols):
        above, below = cut(0, col), cut(last_row, col)
        rows = slice(col * block, (col + 1) * block)
        score_ref[2, rows, :width] = jnp.where(band_even, below, above)
        score_ref[3, rows, :width] = jnp.where(band_even, above, below)
    s1_ref[...] = score_ref[2, : half_cols * block, :width].astype(BF16)
    s2_ref[...] = score_ref[3, : half_cols * block, :width].astype(BF16)
    for s_ref, down_first in (((c11_ref, c12_ref), True), ((c21_ref, c22_ref), False)):
        chosen = band_even if down_first else jnp.logical_not(band_even)
        lefts = jnp.where(chosen, cut(last_row, 0), cut(0, 0))
        rights = jnp.where(chosen, cut(last_row, last_col), cut(0, last_col))
        s_ref[0][...] = jnp.where(lon_even, rights, lefts).astype(BF16)
        s_ref[1][...] = jnp.where(lon_even, lefts, rights).astype(BF16)


def second_kernel(
    normed_ref, latent_ref, l1_ref, l2_ref, s1_ref, s2_ref, c11_ref, c12_ref, c21_ref, c22_ref,
    gains_ref, bias_ref, qkv_hbm, proj_hbm, decode_hbm,
    out_ref, frame_ref, cells_ref, row_ref, qkv_ref, proj_ref, decode_ref, sems,
    *, half_rows, half_cols, head_count, lon_axis, band_axes,
):
    levels = out_ref.shape[0]
    cells, width = normed_ref.shape
    block = levels * HALF_ROWS * HALF_COLS
    run = HALF_ROWS * HALF_COLS
    pairs = ((qkv_hbm.at[1], qkv_ref), (proj_hbm.at[1], proj_ref), (decode_hbm, decode_ref))
    weights = [pltpu.make_async_copy(a, b, sems.at[i]) for i, (a, b) in enumerate(pairs)]
    for copy in weights:
        copy.start()
    lon_even = lax.axis_index(lon_axis) % 2 == 0
    band = lax.axis_index(band_axes)
    band_even = band % 2 == 0
    first_band = band == 0
    last_band = band == lax.axis_size(band_axes) - 1

    right, left = half_cols, -1
    below, above = half_rows, -1
    col1 = jnp.where(lon_even, right, left)
    col2 = jnp.where(lon_even, left, right)
    row1 = jnp.where(band_even, below, above)
    row2 = jnp.where(band_even, above, below)
    chunks = [(normed_ref, [(r, c) for r in range(half_rows) for c in range(half_cols)])]
    chunks += [(l1_ref, [(r, col1) for r in range(half_rows)]), (l2_ref, [(r, col2) for r in range(half_rows)])]
    chunks += [(s1_ref, [(row1, c) for c in range(half_cols)]), (s2_ref, [(row2, c) for c in range(half_cols)])]
    chunks += [(c11_ref, [(row1, col1)]), (c12_ref, [(row1, col2)]), (c21_ref, [(row2, col1)]), (c22_ref, [(row2, col2)])]
    window_cols = half_cols // 2 + 1

    def window_of(row, col):
        return ((row + 1) // 2) * window_cols + (col + 1) // 2

    start = 0
    places = []
    for ref, blocks in chunks:
        size = ref.shape[0]
        frame_ref[start : start + size, :] = ref[...].astype(F32)
        start += size
        places += blocks
    total = start
    key = iota((1, total), 1)
    key_place = key // block
    key_window = jnp.zeros((1, total), jnp.int32)
    for index, (row, col) in enumerate(places):
        window = jnp.asarray(window_of(row, col), jnp.int32)
        if not isinstance(row, int):
            missing = ((row < 0) & first_band) | ((row >= half_rows) & last_band)
            window = jnp.where(missing, -1, window)
        key_window = jnp.where(key_place == index, window, key_window)
    key_id = jnp.where(key_window < 0, -1, key_window * (levels + 1) + ((key % block) // run + WLEV // 2) // WLEV)
    query = iota((cells, 1), 0)
    query_place = query // block
    query_window = window_of(query_place // half_cols, query_place % half_cols)
    query_id = query_window * (levels + 1) + ((query % block) // run + WLEV // 2) // WLEV
    allowed = query_id == key_id

    frame = frame_ref[...].astype(BF16)
    weights[0].wait()
    queries = mm(normed_ref[...], qkv_ref[:, :width]).astype(BF16)
    keys_vals = mm(frame, qkv_ref[:, width:]).astype(BF16)
    context = attend(queries, keys_vals[:, :width], keys_vals[:, width:], allowed, head_count)
    weights[1].wait()
    latent = latent_ref[...] + mm(context, proj_ref[...])
    final = layer_norm(latent, gains_ref[3:4, :]).astype(BF16)
    weights[2].wait()
    cells_ref[...] = mm(final, decode_ref[...]) + bias_ref[...]
    for level in range(levels):
        for row in range(half_rows):
            for step in range(HALF_ROWS):
                for col in range(half_cols):
                    source = (row * half_cols + col) * block + level * run + step * HALF_COLS
                    row_ref[col * HALF_COLS : (col + 1) * HALF_COLS, :] = cells_ref[source : source + HALF_COLS, :]
                out_ref[level, row * HALF_ROWS + step] = row_ref[...].astype(BF16)


def swap_first(index, size):
    return index ^ 1 if (index ^ 1) < size else index


def swap_second(index, size, wrap):
    other = ((index + 1) ^ 1) - 1
    if wrap:
        return other % size
    return other if 0 <= other < size else index


def per_device(
    fields, score_table, score_bias, value_table, value_bias, agg_weight, qkv_weight, proj_weight, up_weight,
    down_weight, norm_gains, decode_weight, decode_bias, *, mesh_shape,
):
    band_axes = ("var", "lat")
    lon_axis = "lon"
    sizes = [mesh_shape[name] for name in ("var", "lon", "lat")]
    bands = sizes[0] * sizes[2]
    local_vars, levels, all_rows, cols, patch = fields.shape
    all_vars, _, head_count = score_table.shape
    width = agg_weight.shape[0]
    hidden_width = up_weight.shape[1]
    out_width = decode_weight.shape[1]
    rows = all_rows // bands
    half_rows, half_cols = rows // HALF_ROWS, cols // HALF_COLS
    cells = levels * rows * cols
    block = levels * HALF_ROWS * HALF_COLS
    features = local_vars * patch
    lanes = LANES
    assert features + BIAS_PARTS * local_vars <= lanes
    vmem = pl.BlockSpec(memory_space=pltpu.VMEM)
    hbm = pl.BlockSpec(memory_space=pltpu.HBM)

    packed = pl.pallas_call(
        pack_kernel,
        out_shape=jax.ShapeDtypeStruct((bands, cells, lanes), BF16),
        in_specs=[vmem],
        out_specs=vmem,
        scratch_shapes=[pltpu.VMEM((bands, cells, lanes), F32)],
        name="pack",
    )(fields.transpose(0, 1, 3, 4, 2))
    received = lax.all_to_all(packed, band_axes, 0, 0, tiled=True)

    side = (half_rows * block, width)
    line = (half_cols * block, width)
    corner = (block, width)
    shapes = [(cells, width), side, side, line, line, corner, corner, corner, corner]
    structs = [jax.ShapeDtypeStruct(s, BF16) for s in shapes]
    structs.insert(1, jax.ShapeDtypeStruct((cells, width), F32))
    normed, latent, *sends = pl.pallas_call(
        functools.partial(
            first_kernel, levels=levels, half_rows=half_rows, half_cols=half_cols, head_count=head_count,
            lon_axis=lon_axis, band_axes=band_axes,
        ),
        out_shape=structs,
        in_specs=[vmem] * 5 + [hbm] * 6,
        out_specs=[vmem] * len(structs),
        scratch_shapes=[
            pltpu.VMEM((bands * lanes, head_count * lanes), BF16),
            pltpu.VMEM((bands, cells, head_count * lanes), F32),
            pltpu.VMEM((lanes - features, width), F32),
            pltpu.VMEM((bands * lanes, width), BF16),
            pltpu.VMEM((width, width), BF16),
            pltpu.VMEM((width, 3 * width), BF16),
            pltpu.VMEM((width, width), BF16),
            pltpu.VMEM((width, hidden_width), BF16),
            pltpu.VMEM((hidden_width, width), BF16),
            pltpu.VMEM((cells, width), F32),
            pltpu.SemaphoreType.DMA((5 + bands,)),
        ],
        name="first",
    )(
        received,
        score_table.transpose(1, 2, 0).reshape(patch * head_count, all_vars),
        score_bias.T,
        value_bias,
        norm_gains,
        value_table.reshape(all_vars * patch, width),
        agg_weight,
        qkv_weight,
        proj_weight,
        up_weight,
        down_weight,
    )

    def swap(array, band_to, lon_to):
        pairs = []
        for var in range(sizes[0]):
            for lon in range(sizes[1]):
                for lat in range(sizes[2]):
                    band = band_to(var * sizes[2] + lat)
                    other = ((band // sizes[2]) * sizes[1] + lon_to(lon)) * sizes[2] + band % sizes[2]
                    pairs.append(((var * sizes[1] + lon) * sizes[2] + lat, other))
        return lax.ppermute(array, ("var", "lon", "lat"), pairs)

    def stay(index):
        return index

    band1 = functools.partial(swap_first, size=bands)
    band2 = functools.partial(swap_second, size=bands, wrap=False)
    lon1 = functools.partial(swap_first, size=sizes[1])
    lon2 = functools.partial(swap_second, size=sizes[1], wrap=True)
    moves = [(stay, lon1), (stay, lon2), (band1, stay), (band2, stay)]
    moves += [(band1, lon1), (band1, lon2), (band2, lon1), (band2, lon2)]
    halos = [swap(array, *move) for array, move in zip(sends, moves, strict=True)]

    total = sum(a.shape[0] for a in halos) + cells
    return pl.pallas_call(
        functools.partial(
            second_kernel, half_rows=half_rows, half_cols=half_cols, head_count=head_count, lon_axis=lon_axis,
            band_axes=band_axes,
        ),
        out_shape=jax.ShapeDtypeStruct((levels, rows, cols, out_width), BF16),
        in_specs=[vmem] * 12 + [hbm] * 3,
        out_specs=vmem,
        scratch_shapes=[
            pltpu.VMEM((total, width), F32),
            pltpu.VMEM((cells, out_width), F32),
            pltpu.VMEM((cols, out_width), F32),
            pltpu.VMEM((width, 3 * width), BF16),
            pltpu.VMEM((width, width), BF16),
            pltpu.VMEM((width, out_width), BF16),
            pltpu.SemaphoreType.DMA((3,)),
        ],
        name="second",
    )(normed, latent, *halos, norm_gains, decode_bias.reshape(1, -1), qkv_weight, proj_weight, decode_weight)


def solution(mesh):
    shape = dict(mesh.shape)
    return jax.shard_map(
        functools.partial(per_device, mesh_shape=shape),
        mesh=mesh,
        in_specs=(P(("var", "lat"), None, None, "lon", None),) + (P(),) * 12,
        out_specs=P(None, ("var", "lat"), "lon", None),
        check_vma=False,
    )
```

time: 321 us -> 53.9 us (0.17)
  local copies, waits for them, and re-layouts: 87.7 us -> 3.13 us
  other arithmetic: 58 us -> 0 us
  waiting for transfers between devices: 54.7 us -> 4.95 us
  blocking collectives: 62.4 us -> 13.1 us
  matrix products: 32.2 us -> 0 us
  Pallas kernels: 0 us -> 20.2 us
  between operations: 14 us -> 0.12 us
  starting transfers between devices: 8.62 us -> 11.9 us
    psum x1 -> x0, waiting for transfers between devices: 49.8 us -> none  [per_device(): lax.psum(numerator.astype(jnp.bfloat16), ('var', 'lat')).astype(jnp.float32)]
    add x12 -> x0, other arithmetic: 48.9 us -> none  [the longest x6 34.3 us: add_var(): totals[0] + weights[..., None] * values]
    psum x1 -> x0, blocking collectives: 34.6 us -> none  [per_device(): lax.psum(denominator.astype(jnp.bfloat16), ('var', 'lat'))]
    reshape x13 -> x1, local copies, waits for them, and re-layouts: 33.6 us -> 0.6 us  [per_device(): decode_bias.reshape(1, -1)]
    dot_general x18 -> x0, matrix products: 30.6 us -> none  [the longest x6 11.3 us: add_var(): jnp.dot(patch.reshape(-1, patch_size), tab, preferred_element_type=jnp.fl...]
    pmax x1 -> x0, blocking collectives: 27.8 us -> none  [per_device(): lax.pmax(jnp.max(scores, axis=0).astype(jnp.bfloat16), ('var', 'lat'))]
    pallas_call x0 -> x3, Pallas kernels: none -> 20.2 us  [the longest x1 9.39 us: per_device(): pl.pallas_call(functools.partial(first_kernel, levels=levels, half_rows=h...]
    dynamic_slice x36 -> x0, local copies, waits for them, and re-layouts: 18.7 us -> none  [the longest x30 15.1 us: group_terms(): sums, _ = lax.scan(add_var, start, (patches, scores, table, offsets))]
  transfers between devices with their start and end apart: 5 -> 8, of which waited for: 3 -> 2; matrix products, arithmetic and copies ran while one was open for 3% -> 1% of each run, Pallas kernels for 0% -> 0%
where the time goes in v1:
time: 53.9 us; the launch traced here: 53.5 us
  Pallas kernels  20.2 us (37%)
  blocking collectives  13.1 us (24%)
  starting transfers between devices  11.9 us (22%)
  waiting for transfers between devices  4.95 us (9%)
  local copies, waits for them, and re-layouts  3.13 us (6%)
    all_to_all x1, blocking collectives, per_device(): received = lax.all_to_all(packed, band_axes, 0, 0, tiled=True)  13.1 us
    ppermute x8, starting transfers between devices, swap(): return lax.ppermute(array, ('var', 'lon', 'lat'), pairs)  11.9 us
    pallas_call x1, Pallas kernels, per_device(): pl.pallas_call(functools.partial(first_kernel, levels=levels, half_rows=h...  9.39 us
    pallas_call x1, Pallas kernels, per_device(): pl.pallas_call(functools.partial(second_kernel, half_rows=half_rows, half...  8.19 us
    ppermute x8, waiting for transfers between devices, swap(): return lax.ppermute(array, ('var', 'lon', 'lat'), pairs)  4.95 us
    pallas_call x1, Pallas kernels, per_device(): pl.pallas_call(pack_kernel, out_shape=jax.ShapeDtypeStruct((bands, cells,...  2.61 us
    pallas_call x1, local copies, waits for them, and re-layouts, per_device(): pl.pallas_call(functools.partial(second_kernel, half_rows=half_rows, half...  1.88 us
  transfers between devices with their start and end apart: 8, of which 2 were waited for; matrix products, arithmetic and copies ran while one was open for 1% of the time, Pallas kernels for 0%

profile of v1, /device:TPU:11, one launch (start us, length us, event | category | flops | bytes accessed | tf_op | source)
XLA Modules:
  0.0 53.5 jit_solution(7096048065384335483)
XLA Ops:
  0.0 2.6 %pack.1 = bf16[8,144,128]{2,1,0:T(8,128)(2,1)} custom-call(bf16[6,2,12,16,48]{4,3,2,1,0:T(8,128)(2,1)} %bitcast.7), custom_call_target="tpu_custom_call" | custom-call | tf_op jit(solution)/shard_map/pack/pallas_call | solution.py:389
  2.6 13.1 %all_to_all.5.received_ref = bf16[8,144,128]{2,1,0:T(8,128)(2,1)} all-to-all(bf16[8,144,128]{2,1,0:T(8,128)(2,1)} %pack.1), channel_id=1, replica_groups=mesh['var'=4,'lon'=4,'lat'=2] {'var','lat'}, dimensions={0} | all-to-all | bytes 589824 | tf_op jit(solution)/shard_map/all_to_all | solution.py:397
  15.8 0.0 copy-start.8
  15.8 9.4 %first.1 = (bf16[144,512]{1,0:T(8,128)(2,1)}, f32[144,512]{1,0:T(8,128)}, bf16[72,512]{1,0:T(8,128)(2,1)}, bf16[72,512]{1,0:T(8,128)(2,1)}, bf16[72,512]{1,0:T(8...) custom-call(bf16[8,144,128]{2,1,0:T(8,128)(2,1)} %all_to_all.5.recei, ...), custom_call_target="tpu_custom_call" | custom-call | tf_op jit(solution)/shard_map/first/pallas_call | solution.py:405
  25.2 3.1 %collective-permute-start.4 = (bf16[36,512]{1,0:T(8,128)(2,1)}, bf16[36,512]{1,0:T(8,128)(2,1)S(1)}, u32[]{:S(2)}, u32[]{:S(2)}) collective-permute-start(bf16[36,512]{1,0:T(8,128)(2,1)} %get-tuple-element.21), channel_id=1, source_target_pairs={{0,3},{1,2},{2,1},{3,0},{4,7},{5,6},{6,5},{7,4},{8,11},{9,10},{10,... | collective-permute-start | bytes 110600 | tf_op jit(solution)/shard_map/ppermute | solution.py:449
  28.2 0.1 collective-permute-start.5
  28.3 1.5 %collective-permute-start = (bf16[72,512]{1,0:T(8,128)(2,1)}, bf16[72,512]{1,0:T(8,128)(2,1)S(1)}, u32[]{:S(2)}, u32[]{:S(2)}) collective-permute-start(bf16[72,512]{1,0:T(8,128)(2,1)} %get-tuple-element.17), channel_id=1, source_target_pairs={{0,2},{1,3},{2,0},{3,1},{4,6},{5,7},{6,4},{7,5},{8,10},{9,11},{10,... | collective-permute-start | bytes 221192 | tf_op jit(solution)/shard_map/ppermute | solution.py:449
  29.8 1.1 %collective-permute-start.1 = (bf16[72,512]{1,0:T(8,128)(2,1)}, bf16[72,512]{1,0:T(8,128)(2,1)S(1)}, u32[]{:S(2)}, u32[]{:S(2)}) collective-permute-start(bf16[72,512]{1,0:T(8,128)(2,1)} %get-tuple-element.18), channel_id=1, source_target_pairs={{0,6},{1,7},{2,4},{3,5},{4,2},{5,3},{6,0},{7,1},{8,14},{9,15},{10,... | collective-permute-start | bytes 221192 | tf_op jit(solution)/shard_map/ppermute | solution.py:449
  30.9 1.6 %collective-permute-start.6 = (bf16[36,512]{1,0:T(8,128)(2,1)}, bf16[36,512]{1,0:T(8,128)(2,1)S(1)}, u32[]{:S(2)}, u32[]{:S(2)}) collective-permute-start(bf16[36,512]{1,0:T(8,128)(2,1)} %get-tuple-element.23), channel_id=1, source_target_pairs={{0,2},{1,10},{2,0},{3,8},{4,6},{5,14},{6,4},{7,12},{8,3},{9,18},{1... | collective-permute-start | bytes 110600 | tf_op jit(solution)/shard_map/ppermute | solution.py:449
  32.5 0.0 collective-permute-done.4.c11_ref
  32.5 0.0 copy-start.4
  32.5 0.2 collective-permute-start.2
  32.8 0.4 collective-permute-done.5.c12_ref
  33.2 0.0 copy-start.5
  33.2 3.9 %collective-permute-start.3 = (bf16[72,512]{1,0:T(8,128)(2,1)}, bf16[72,512]{1,0:T(8,128)(2,1)S(1)}, u32[]{:S(2)}, u32[]{:S(2)}) collective-permute-start(bf16[72,512]{1,0:T(8,128)(2,1)} %get-tuple-element.20), channel_id=1, source_target_pairs={{0,0},{1,8},{2,2},{3,10},{4,4},{5,12},{6,6},{7,14},{8,1},{9,16},{1... | collective-permute-start | bytes 221192 | tf_op jit(solution)/shard_map/ppermute | solution.py:449
  37.1 0.0 collective-permute-done.6.c21_ref
  37.1 0.0 copy-start.6
  37.2 0.4 collective-permute-start.7
  37.5 0.0 copy-done.8
  37.6 0.6 %reshape.11.bias_ref = f32[1,768]{1,0:T(1,128)} reshape(f32[768]{0:T(1024)S(1)} %copy-done.8) | data formatting | bytes 6144 | tf_op jit(solution)/shard_map/reshape | solution.py:481
  38.1 4.5 %collective-permute-done.7.c22_ref = bf16[36,512]{1,0:T(8,128)(2,1)S(1)} collective-permute-done((bf16[36,512]{1,0:T(8,128)(2,1)}, bf16[36,512]{1,0:T(8,128)(2,1)S(1)}, u32[]{:S(2)}, u32[]{:S(2)}) %collective-permute-start.7) | collective-permute-done | bytes 36896 | tf_op jit(solution)/shard_map/ppermute | solution.py:449
  42.7 0.0 copy-start.7
  42.7 0.0 collective-permute-done.l1_ref
  42.7 0.0 copy-start
  42.7 0.0 collective-permute-done.1.l2_ref
  42.7 0.0 copy-start.1
  42.7 0.0 collective-permute-done.2.s1_ref
  42.7 0.0 copy-start.2
  42.7 0.0 collective-permute-done.3.s2_ref
  42.7 0.0 copy-start.3
  42.7 0.0 copy-done.4
  42.7 0.0 copy-done.5
  42.7 0.0 copy-done.6
  42.8 0.5 copy-done.7
  43.3 0.0 copy-done
  43.3 0.0 copy-done.1
  43.3 0.0 copy-done.2
  43.4 0.0 copy-done.3
  43.4 8.2 %second.1 = bf16[2,6,12,768]{3,2,1,0:T(8,128)(2,1)} custom-call(bf16[144,512]{1,0:T(8,128)(2,1)} %get-tuple-element.15.normed_ref, f32[144,512]{1,0:T(8,128)} %get-tuple-element.16.latent_ref, bf16[72,512]{1,0:T(8,128)(2,1)} %copy-done, bf16[72,512]{1,0:T(8,128)(2,1)} %copy-done.1, bf16[72,512]{1,0:T(8,128)(2,1)} %copy-done.2, bf16[72,512]{1,0:T(8,128)(2,1)} %copy-done.3, ...), custom_call_target="tpu_custom_call" | custom-call | tf_op jit(solution)/shard_map/second/pallas_call | solution.py:463
  51.6 1.9 %copy.14 = bf16[2,6,12,768]{3,0,2,1:T(2,128)(2,1)} copy(bf16[2,6,12,768]{3,2,1,0:T(8,128)(2,1)} %second.1) | data formatting | bytes 442368 | tf_op jit(solution)/shard_map/second/pallas_call | solution.py:463
Async XLA Ops:
  15.8 21.8 %copy-start.8 = (f32[768]{0:T(1024)S(1)}, f32[768]{0:T(1024)}, u32[]{:S(2)}) copy-start(f32[768]{0:T(1024)} %param.25) | copy-start | bytes 9220
  25.2 7.4 %collective-permute-start.4 = (bf16[36,512]{1,0:T(8,128)(2,1)}, bf16[36,512]{1,0:T(8,128)(2,1)S(1)}, u32[]{:S(2)}, u32[]{:S(2)}) collective-permute-start(bf16[36,512]{1,0:T(8,128)(2,1)} %get-tuple-element.21), channel_id=1, source_target_pairs={{0,3},{1,2},{2,1},{3,0},{4,7},{5,6},{6,5},{7,4},{8,11},{9,10},{10,... | collective-permute-start | bytes 110600 | tf_op jit(solution)/shard_map/ppermute | solution.py:449
  28.2 5.0 %collective-permute-start.5 = (bf16[36,512]{1,0:T(8,128)(2,1)}, bf16[36,512]{1,0:T(8,128)(2,1)S(1)}, u32[]{:S(2)}, u32[]{:S(2)}) collective-permute-start(bf16[36,512]{1,0:T(8,128)(2,1)} %get-tuple-element.22), channel_id=1, source_target_pairs={{0,7},{1,6},{2,5},{3,4},{4,3},{5,2},{6,1},{7,0},{8,15},{9,14},{10,... | collective-permute-start | bytes 110600 | tf_op jit(solution)/shard_map/ppermute | solution.py:449
  28.3 14.4 %collective-permute-start = (bf16[72,512]{1,0:T(8,128)(2,1)}, bf16[72,512]{1,0:T(8,128)(2,1)S(1)}, u32[]{:S(2)}, u32[]{:S(2)}) collective-permute-start(bf16[72,512]{1,0:T(8,128)(2,1)} %get-tuple-element.17), channel_id=1, source_target_pairs={{0,2},{1,3},{2,0},{3,1},{4,6},{5,7},{6,4},{7,5},{8,10},{9,11},{10,... | collective-permute-start | bytes 221192 | tf_op jit(solution)/shard_map/ppermute | solution.py:449
  29.8 12.9 %collective-permute-start.1 = (bf16[72,512]{1,0:T(8,128)(2,1)}, bf16[72,512]{1,0:T(8,128)(2,1)S(1)}, u32[]{:S(2)}, u32[]{:S(2)}) collective-permute-start(bf16[72,512]{1,0:T(8,128)(2,1)} %get-tuple-element.18), channel_id=1, source_target_pairs={{0,6},{1,7},{2,4},{3,5},{4,2},{5,3},{6,0},{7,1},{8,14},{9,15},{10,... | collective-permute-start | bytes 221192 | tf_op jit(solution)/shard_map/ppermute | solution.py:449
  30.9 6.2 %collective-permute-start.6 = (bf16[36,512]{1,0:T(8,128)(2,1)}, bf16[36,512]{1,0:T(8,128)(2,1)S(1)}, u32[]{:S(2)}, u32[]{:S(2)}) collective-permute-start(bf16[36,512]{1,0:T(8,128)(2,1)} %get-tuple-element.23), channel_id=1, source_target_pairs={{0,2},{1,10},{2,0},{3,8},{4,6},{5,14},{6,4},{7,12},{8,3},{9,18},{1... | collective-permute-start | bytes 110600 | tf_op jit(solution)/shard_map/ppermute | solution.py:449
  32.5 10.2 %copy-start.4 = (bf16[36,512]{1,0:T(8,128)(2,1)}, bf16[36,512]{1,0:T(8,128)(2,1)S(1)}, u32[]{:S(2)}) copy-start(bf16[36,512]{1,0:T(8,128)(2,1)S(1)} %collective-permute-done.4.c11_ref) | copy-start | bytes 110596
  32.5 10.2 %collective-permute-start.2 = (bf16[72,512]{1,0:T(8,128)(2,1)}, bf16[72,512]{1,0:T(8,128)(2,1)S(1)}, u32[]{:S(2)}, u32[]{:S(2)}) collective-permute-start(bf16[72,512]{1,0:T(8,128)(2,1)} %get-tuple-element.19), channel_id=1, source_target_pairs={{0,1},{1,0},{2,3},{3,2},{4,5},{5,4},{6,7},{7,6},{8,9},{9,8},{10,11... | collective-permute-start | bytes 221192 | tf_op jit(solution)/shard_map/ppermute | solution.py:449
  33.2 9.5 %copy-start.5 = (bf16[36,512]{1,0:T(8,128)(2,1)}, bf16[36,512]{1,0:T(8,128)(2,1)S(1)}, u32[]{:S(2)}) copy-start(bf16[36,512]{1,0:T(8,128)(2,1)S(1)} %collective-permute-done.5.c12_ref) | copy-start | bytes 110596
  33.2 9.5 %collective-permute-start.3 = (bf16[72,512]{1,0:T(8,128)(2,1)}, bf16[72,512]{1,0:T(8,128)(2,1)S(1)}, u32[]{:S(2)}, u32[]{:S(2)}) collective-permute-start(bf16[72,512]{1,0:T(8,128)(2,1)} %get-tuple-element.20), channel_id=1, source_target_pairs={{0,0},{1,8},{2,2},{3,10},{4,4},{5,12},{6,6},{7,14},{8,1},{9,16},{1... | collective-permute-start | bytes 221192 | tf_op jit(solution)/shard_map/ppermute | solution.py:449
  37.1 5.6 %copy-start.6 = (bf16[36,512]{1,0:T(8,128)(2,1)}, bf16[36,512]{1,0:T(8,128)(2,1)S(1)}, u32[]{:S(2)}) copy-start(bf16[36,512]{1,0:T(8,128)(2,1)S(1)} %collective-permute-done.6.c21_ref) | copy-start | bytes 110596
  37.2 5.5 %collective-permute-start.7 = (bf16[36,512]{1,0:T(8,128)(2,1)}, bf16[36,512]{1,0:T(8,128)(2,1)S(1)}, u32[]{:S(2)}, u32[]{:S(2)}) collective-permute-start(bf16[36,512]{1,0:T(8,128)(2,1)} %get-tuple-element.24), channel_id=1, source_target_pairs={{0,6},{1,14},{2,4},{3,12},{4,2},{5,10},{6,0},{7,8},{8,7},{9,22},{1... | collective-permute-start | bytes 110600 | tf_op jit(solution)/shard_map/ppermute | solution.py:449
  42.7 0.6 %copy-start.7 = (bf16[36,512]{1,0:T(8,128)(2,1)}, bf16[36,512]{1,0:T(8,128)(2,1)S(1)}, u32[]{:S(2)}) copy-start(bf16[36,512]{1,0:T(8,128)(2,1)S(1)} %collective-permute-done.7.c22_ref) | copy-start | bytes 110596
  42.7 0.6 %copy-start = (bf16[72,512]{1,0:T(8,128)(2,1)}, bf16[72,512]{1,0:T(8,128)(2,1)S(1)}, u32[]{:S(2)}) copy-start(bf16[72,512]{1,0:T(8,128)(2,1)S(1)} %collective-permute-done.l1_ref) | copy-start | bytes 221188
  42.7 0.7 %copy-start.1 = (bf16[72,512]{1,0:T(8,128)(2,1)}, bf16[72,512]{1,0:T(8,128)(2,1)S(1)}, u32[]{:S(2)}) copy-start(bf16[72,512]{1,0:T(8,128)(2,1)S(1)} %collective-permute-done.1.l2_ref) | copy-start | bytes 221188
  42.7 0.7 %copy-start.2 = (bf16[72,512]{1,0:T(8,128)(2,1)}, bf16[72,512]{1,0:T(8,128)(2,1)S(1)}, u32[]{:S(2)}) copy-start(bf16[72,512]{1,0:T(8,128)(2,1)S(1)} %collective-permute-done.2.s1_ref) | copy-start | bytes 221188
  42.7 0.7 %copy-start.3 = (bf16[72,512]{1,0:T(8,128)(2,1)}, bf16[72,512]{1,0:T(8,128)(2,1)S(1)}, u32[]{:S(2)}) copy-start(bf16[72,512]{1,0:T(8,128)(2,1)S(1)} %collective-permute-done.3.s2_ref) | copy-start | bytes 221188
